TPU v7x, 256 devices: a whole 4x4x8 slice. The times are simulated.
256 devices in a mesh: tm: 64 (over y, x, z_lo), chan: 4 (over z_hi, core).
Axes of the slice: x: 4, y: 4, z: 8 (z_hi: 2, z_lo: 4; z = z_hi * 4 + z_lo), core: 2. Of those that a mesh axis runs over, the one named last changes fastest.
Arguments:
- inputs: bfloat16 [32768, 8192], P('tm', 'chan'), may hold values from -52 to 52
- gate_logits: bfloat16 [32768, 8192], P(('tm', 'chan')), may hold values from -5 to 5
- step_sizes: bfloat16 [32768, 64], P('tm', 'chan'), may hold values from 0.3 to 229376, as said below
- decay_rates: float32 [8192], replicated, as said below
- skip_gain: float32 [8192], replicated, may hold values from 0.3 to 0.8
- norm_gain: float32 [8192], replicated, may hold values from 0.25 to 1.75
Outputs:
- outputs: bfloat16 [32768, 8192], P(('tm', 'chan'))
Inputs may be any that keep to these rules, and one draw needn't show every extreme that they name: `step_sizes`: every step size is positive. `decay_rates`: every rate is positive.
All inputs are finite; a program needn't handle non-finite values.
Results may differ from a plain program's by a relative error of at most 0.0049.
Values may be sent and summed in bfloat16 or wider, within the bound.
A program may use at most 64 MiB of HBM per device.

v0:
```python
import jax
import jax.numpy as jnp
from jax import lax
from jax.sharding import PartitionSpec as P

norm_epsilon = 1e-05


def from_everyone(value, axis):
    count = lax.axis_size(axis)
    return lax.all_to_all(
        jnp.broadcast_to(value[None], (count, *value.shape)), axis, 0, 0, tiled=True
    )


def collected_together(value, axis):
    leaves = jax.tree.leaves(value)
    order = sorted(range(len(leaves)), key=lambda k: -leaves[k].size)
    width = (1, *leaves[order[0]].shape)[-1]
    lines = [
        jnp.pad(leaves[k].reshape(-1), (0, -leaves[k].size % width)).reshape(-1, width)
        for k in order
    ]
    both, at, found = (from_everyone(jnp.concatenate(lines), axis), 0, {})
    for k, line in zip(order, lines):
        slab = both[:, at : at + len(line)].reshape(len(both), -1)
        found[k] = slab[:, : leaves[k].size].reshape(-1, *leaves[k].shape)
        at += len(line)
    numbers = iter(range(len(leaves)))
    return jax.tree.map(lambda _: found[next(numbers)], value)


def folded_in_pairs(pieces, combine):
    while len(jax.tree.leaves(pieces)[0]) > 1:
        pieces = jax.vmap(combine)(
            *(jax.tree.map(lambda part: part[side::2], pieces) for side in (0, 1))
        )
    return jax.tree.map(lambda part: part[0], pieces)


def carried_in(value, axis, combine, identity):
    count, mine = (lax.axis_size(axis), lax.axis_index(axis))
    passed = jnp.arange(count) < mine

    def kept(part, zero, own):
        part = jnp.where(
            passed.reshape(-1, *(1 for _ in own.shape)), part, jnp.asarray(zero, own.dtype)
        )
        return part

    pieces = collected_together(value, axis)
    return folded_in_pairs(jax.tree.map(kept, pieces, identity, value), combine)


def combine_pairs(earlier, later):
    return (earlier[0] * later[0], later[0] * earlier[1] + later[1])


def widen(head_values, channels):
    head_count = head_values.shape[1]
    width_each = channels // head_count
    owner = lax.broadcasted_iota(jnp.int32, (head_count, channels), 1) // width_each
    column_head = lax.broadcasted_iota(jnp.int32, (head_count, channels), 0)
    spread_table = (owner == column_head).astype(jnp.float32)
    return jnp.dot(head_values, spread_table, preferred_element_type=jnp.float32)


def serial_rows(decays, drives, axis_pos):
    length = decays.shape[axis_pos]
    prod_list = []
    state_list = []
    prod_now = None
    state_now = None
    for index in range(length):
        decay_here = lax.index_in_dim(decays, index, axis_pos, keepdims=False)
        drive_here = lax.index_in_dim(drives, index, axis_pos, keepdims=False)
        if index == 0:
            prod_now = decay_here
            state_now = drive_here
        else:
            prod_now = prod_now * decay_here
            state_now = decay_here * state_now + drive_here
        prod_list.append(prod_now)
        state_list.append(state_now)
    return (jnp.stack(prod_list, axis=axis_pos), jnp.stack(state_list, axis=axis_pos))


def prefix_rows(decays, drives):
    length = decays.shape[0]
    channels = decays.shape[1]
    if length <= 8:
        return serial_rows(decays, drives, 0)
    group = 8
    groups = length // group
    grouped_decay = decays.reshape(groups, group, channels)
    grouped_drive = drives.reshape(groups, group, channels)
    inner_prod, inner_state = serial_rows(grouped_decay, grouped_drive, 1)
    outer_prod, outer_state = prefix_rows(inner_prod[:, -1, :], inner_state[:, -1, :])
    before_prod = jnp.concatenate([jnp.ones((1, channels), jnp.float32), outer_prod[:-1]], axis=0)
    before_state = jnp.concatenate(
        [jnp.zeros((1, channels), jnp.float32), outer_state[:-1]], axis=0
    )
    products = inner_prod * before_prod[:, None, :]
    states = inner_state + inner_prod * before_state[:, None, :]
    return (products.reshape(length, channels), states.reshape(length, channels))


def chain_time(end_decay, end_state):
    identity = (jnp.ones_like(end_decay), jnp.zeros_like(end_state))
    return carried_in((end_decay, end_state), "tm", combine_pairs, identity)[1]


def recurrence(block_inputs, block_steps, rates_here, skip_here, chain_fn):
    channels = block_inputs.shape[1]
    step_values = block_steps.astype(jnp.float32)
    widened = widen(step_values, channels) * rates_here[None, :]
    decays = jnp.exp(-widened)
    values = block_inputs.astype(jnp.float32)
    drives = jnp.sqrt(-jnp.expm1(-2.0 * widened)) * values
    running = jnp.cumsum(step_values, axis=0)
    remaining = widen(running[-1:, :] - running, channels) * rates_here[None, :]
    end_state = jnp.sum(jnp.exp(-remaining) * drives, axis=0)
    end_decay = jnp.exp(-widen(running[-1:, :], channels)[0] * rates_here)
    incoming = chain_fn(end_decay, end_state)
    products, local_states = prefix_rows(decays, drives)
    states = local_states + products * incoming[None, :]
    return (states + skip_here[None, :] * values).astype(jnp.bfloat16)


def normalize(mixed_rows, gate_logits, norm_gain):
    gated = mixed_rows.astype(jnp.float32) * jax.nn.silu(gate_logits.astype(jnp.float32))
    factor = lax.rsqrt(jnp.mean(gated * gated, axis=1, keepdims=True) + norm_epsilon)
    return (gated * factor * norm_gain[None, :]).astype(jnp.bfloat16)


def per_device(inputs, gate_logits, step_sizes, decay_rates, skip_gain, norm_gain):
    channels = inputs.shape[1]
    offset = lax.axis_index("chan") * channels
    rates_here = lax.dynamic_slice_in_dim(decay_rates, offset, channels, 0)
    skip_here = lax.dynamic_slice_in_dim(skip_gain, offset, channels, 0)
    mixed_rows = recurrence(inputs, step_sizes, rates_here, skip_here, chain_time)
    framed = lax.all_to_all(mixed_rows, "chan", split_axis=0, concat_axis=1, tiled=True)
    return normalize(framed, gate_logits, norm_gain)


def solution(mesh):
    in_specs = (P("tm", "chan"), P(("tm", "chan"), None), P("tm", "chan"), P(), P(), P())
    out_specs = P(("tm", "chan"), None)
    return jax.shard_map(
        per_device, mesh=mesh, in_specs=in_specs, out_specs=out_specs, check_vma=False
    )
```

profile of v0, /device:TPU:2, one launch (start us, length us, event | category | flops | bytes accessed | tf_op | source)
XLA Modules:
  0.0 162.5 jit_solution(8134235328284120431)
XLA Ops:
  0.0 0.9 copy_bitcast_fusion.3
  0.9 1.1 reduce-window.6
  2.5 3.4 %fusion.10 = f32[2048,512]{0,1:T(8,128)} fusion(bf16[512,16]{0,1:T(8,128)(2,1)} %param.8, s32[2048]{0:T(1024)S(1)} %get-tuple-element.65, s32[2048]{0:T(1024)S(1)} %get-tuple-element.66, pred[2048]{0:T(1024)(128)(4,1)S(1)} %fusion.30), kind=kOutput, calls=%fused_computation.43 | convolution fusion | flops 33619968 | bytes 4229120 | tf_op jit(solution)/shard_map/dot_general | solution.py:65
  6.8 5.9 %multiply_reduce_fusion.1 = f32[2048]{0:T(1024)S(1)} fusion(f32[2048]{0:T(1024)S(1)} %get-tuple-element.32, bf16[512,2048]{1,0:T(8,128)(2,1)S(1)} %copy-done.2, f32[2048,512]{0,1:T(8,128)} %fusion.10, s32[2048]{0:T(1024)S(1)} %get-tuple-element.65, s32[2048]{0:T(1024)S(1)} %get-tuple-element.66, pred[2048]{0:T(1024)(128)(4,1)S(1)} %fusion.30, ...), kind=kOutput, calls=%fused_computation.15 | convolution fusion | flops 43071488 | bytes 6359360 | tf_op jit(solution)/shard_map/dot_general | solution.py:65
  12.6 1.5 broadcast_in_dim.21
  14.1 12.3 %all-to-all-start = ((f32[64,2,2048]{2,1,0:T(2,128)}), f32[64,2,2048]{2,1,0:T(2,128)}, u32[]{:S(2)}, u32[]{:S(2)}) async-start(f32[64,2,2048]{2,1,0:T(2,128)} %broadcast_in_dim.21), calls=%async_computation | async-start | bytes 2097152 | tf_op jit(solution)/shard_map/all_to_all | solution.py:11
  26.5 2.9 %exponential_bitcast_fusion = f32[64,8,2048]{2,1,0:T(8,128)S(1)} fusion(f32[2048,512]{0,1:T(8,128)} %fusion.10, f32[2048]{0:T(1024)S(1)} %get-tuple-element.32), kind=kLoop, calls=%fused_computation.16 | loop fusion | flops 2097152 | bytes 8396800 | tf_op jit(solution)/shard_map/reshape | solution.py:95
  29.9 2.7 %fusion.7 = f32[64,8,2048]{2,1,0:T(8,128)S(1)} fusion(bf16[512,2048]{1,0:T(8,128)(2,1)S(1)} %copy-done.2, f32[2048,512]{0,1:T(8,128)S(1)} %copy-done, f32[2048]{0:T(1024)S(1)} %get-tuple-element.32), kind=kLoop, calls=%fused_computation.17 | loop fusion | flops 5242880 | bytes 10493952 | tf_op jit(solution)/shard_map/reshape | solution.py:96
  32.6 4.8 %slice_multiply_fusion = (f32[64,1,2048]{2,1,0:T(1,128)S(1)}, f32[64,1,2048]{2,1,0:T(1,128)}, f32[64,1,2048]{2,1,0:T(1,128)}, f32[64,1,2048]{2,1,0:T(1,128)}, f3...) fusion(f32[64,8,2048]{2,1,0:T(8,128)S(1)} %exponential_bitcast_fusion), kind=kLoop, calls=%fused_computation.32 | loop fusion | flops 917504 | bytes 7864320 | tf_op jit(solution)/shard_map/mul | solution.py:81
  37.4 8.4 %slice_add_fusion = (f32[64,1,2048]{2,1,0:T(1,128)S(1)}, f32[64,1,2048]{2,1,0:T(1,128)}, f32[64,1,2048]{2,1,0:T(1,128)}, f32[64,1,2048]{2,1,0:T(1,128)}, f32[64,...) fusion(f32[64,8,2048]{2,1,0:T(8,128)S(1)} %fusion.7, ...), kind=kLoop, calls=%fused_computation.18 | loop fusion | flops 1835008 | bytes 13107200 | tf_op jit(solution)/shard_map/add | solution.py:82
  46.2 1.0 slice_multiply_fusion.7
  47.2 1.4 slice_add_fusion.7
  48.6 2.3 %stack.10 = f32[8,8,2048]{2,1,0:T(8,128)} concatenate(f32[8,1,2048]{2,1,0:T(1,128)} %get-tuple-element.54, f32[8,1,2048]{2,1,0:T(1,128)} %get-tuple-element.17, f32[8,1,2048]{2,1,0:T(1,128)} %get-tuple-element.16, f32[8,1,2048]{2,1,0:T(1,128)} %get-tuple-element.15, f32[8,1,2048]{2,1,0:T(1,128)S(1)} %get-tuple-element.14, f32[8,1,2048]{2,1,0:T(1,128)S(1)} %get-tuple-element.13, ...), dimensions={1} | concatenate | bytes 1048576 | tf_op jit(solution)/shard_map/stack | solution.py:85
  50.9 2.3 %stack.11 = f32[8,8,2048]{2,1,0:T(8,128)} concatenate(f32[8,1,2048]{2,1,0:T(1,128)S(1)} %get-tuple-element.53, f32[8,1,2048]{2,1,0:T(1,128)} %get-tuple-element.30, f32[8,1,2048]{2,1,0:T(1,128)} %get-tuple-element.29, f32[8,1,2048]{2,1,0:T(1,128)} %get-tuple-element.28, f32[8,1,2048]{2,1,0:T(1,128)} %get-tuple-element.27, f32[8,1,2048]{2,1,0:T(1,128)} %get-tuple-element.26, ...), dimensions={1} | concatenate | bytes 1048576 | tf_op jit(solution)/shard_map/stack | solution.py:85
  53.5 1.3 add_bitcast_fusion
  54.8 0.8 concatenate.16
  55.7 0.9 concatenate.18
  56.5 11.9 %stack.8 = f32[64,8,2048]{2,1,0:T(8,128)} concatenate(f32[64,1,2048]{2,1,0:T(1,128)} %get-tuple-element.48, f32[64,1,2048]{2,1,0:T(1,128)} %get-tuple-element.39, f32[64,1,2048]{2,1,0:T(1,128)} %get-tuple-element.38, f32[64,1,2048]{2,1,0:T(1,128)} %get-tuple-element.37, f32[64,1,2048]{2,1,0:T(1,128)} %get-tuple-element.36, f32[64,1,2048]{2,1,0:T(1,128)} %get-tuple-element.35, ...), dimensions={1} | concatenate | bytes 8388608 | tf_op jit(solution)/shard_map/stack | solution.py:85
  68.4 11.9 %stack.9 = f32[64,8,2048]{2,1,0:T(8,128)} concatenate(f32[64,1,2048]{2,1,0:T(1,128)} %get-tuple-element.47, f32[64,1,2048]{2,1,0:T(1,128)} %get-tuple-element.46, f32[64,1,2048]{2,1,0:T(1,128)} %get-tuple-element.45, f32[64,1,2048]{2,1,0:T(1,128)} %get-tuple-element.44, f32[64,1,2048]{2,1,0:T(1,128)} %get-tuple-element.43, f32[64,1,2048]{2,1,0:T(1,128)} %get-tuple-element.42, ...), dimensions={1} | concatenate | bytes 8388608 | tf_op jit(solution)/shard_map/stack | solution.py:85
  80.4 2.7 %fusion.49 = (f32[64,1,2048]{2,1,0:T(1,128)S(1)}, f32[64,1,2048]{2,1,0:T(1,128)S(1)}) fusion(f32[64,2,2048]{2,1,0:T(2,128)} %all-to-all-done), kind=kLoop, calls=%fused_computation.119 | loop fusion | bytes 2097152 | tf_op jit(solution)/shard_map/slice | solution.py:26
  83.5 0.8 slice.285
  85.1 0.8 slice.297
  85.9 0.8 slice.296
  86.7 2.0 %fusion.50 = (f32[32,2048]{1,0:T(8,128)}, f32[32,2048]{1,0:T(8,128)S(1)}) fusion(f32[32,2048]{1,0:T(8,128)} %slice.284, f32[32,2048]{1,0:T(8,128)} %slice.285, f32[32,2048]{1,0:T(8,128)} %slice.297, f32[32,2048]{1,0:T(8,128)} %slice.296), kind=kLoop, calls=%fused_computation.120 | loop fusion | flops 196608 | bytes 1572864 | tf_op jit(solution)/shard_map/vmap()/mul | solution.py:56
  88.7 1.0 slice.287
  89.7 1.6 slice.286
  92.7 1.1 fusion.51
  94.2 4.3 %fusion.1 = bf16[512,2048]{1,0:T(8,128)(2,1)S(1)} fusion(bf16[512,2048]{1,0:T(8,128)(2,1)S(1)} %copy-done.2, f32[64,8,2048]{2,1,0:T(8,128)} %stack.9, f32[64,8,2048]{2,1,0:T(8,128)} %stack.8, f32[2048]{0:T(1024)S(1)} %dynamic-slice-done, f32[2048]{0:T(1024)S(1)} %bitcast.175, f32[64,2048]{1,0:T(8,128)S(1)} %copy-done.4, f32[64,2048]{1,0:T(8,128)S(1)} %copy-done.3), kind=kLoop, calls=%fused_computation.5 | loop fusion | flops 9437184 | bytes 13647872 | tf_op jit(solution)/shard_map/convert_element_type | solution.py:127
  98.5 57.6 %all_to_all.18 = bf16[4,128,2048]{2,1,0:T(8,128)(2,1)S(1)} all-to-all(bf16[4,128,2048]{2,1,0:T(8,128)(2,1)S(1)} %bitcast.168), channel_id=1, replica_groups=mesh['tm'=64,'chan'=4] {'chan'}, dimensions={0} | all-to-all | bytes 4194304 | tf_op jit(solution)/shard_map/all_to_all | solution.py:142
  157.0 1.3 copy-done.1
  158.3 1.5 multiply_reduce_fusion
  159.7 2.8 %multiply_convert_fusion = bf16[128,8192]{1,0:T(8,128)(2,1)} fusion(f32[8192]{0:T(1024)S(1)} %copy-done.5, f32[128]{0:T(128)S(1)} %add_rsqrt_fusion, f32[128,8192]{1,0:T(8,128)S(1)} %bitcast.167, bf16[128,8192]{1,0:T(8,128)(2,1)S(1)} %copy-done.1), kind=kLoop, calls=%fused_computation.13 | loop fusion | flops 9437184 | bytes 8421888 | tf_op jit(solution)/shard_map/convert_element_type | solution.py:133
  (58 shorter events, 6.4 us)
Async XLA Ops:
  0.0 6.8 %copy-start.2 = (bf16[512,2048]{1,0:T(8,128)(2,1)S(1)}, bf16[512,2048]{1,0:T(8,128)(2,1)}, u32[]{:S(2)}) copy-start(bf16[512,2048]{1,0:T(8,128)(2,1)} %param.6) | copy-start | bytes 6291460
  14.1 66.2 %all-to-all-start = ((f32[64,2,2048]{2,1,0:T(2,128)}), f32[64,2,2048]{2,1,0:T(2,128)}, u32[]{:S(2)}, u32[]{:S(2)}) async-start(f32[64,2,2048]{2,1,0:T(2,128)} %broadcast_in_dim.21), calls=%async_computation | async-start | bytes 2097152 | tf_op jit(solution)/shard_map/all_to_all | solution.py:11
  26.4 3.5 %copy-start = (f32[2048,512]{0,1:T(8,128)S(1)}, f32[2048,512]{0,1:T(8,128)}, u32[]{:S(2)}) copy-start(f32[2048,512]{0,1:T(8,128)} %fusion.10) | copy-start | bytes 12582916
  83.1 11.1 %dynamic-slice-start = ((f32[8192]{0:T(1024)}, s32[]{:T(128)}), f32[2048]{0:T(1024)S(1)}, s32[]{:S(2)}) async-start(f32[8192]{0:T(1024)} %param.10, s32[]{:T(128)} %select_n.23), calls=%async_computation.2 | async-start | bytes 16896 | tf_op jit(solution)/shard_map/dynamic_slice | solution.py:140
  85.1 9.1 %copy-start.3 = (f32[64,2048]{1,0:T(8,128)S(1)}, f32[64,2048]{1,0:T(8,128)}, u32[]{:S(2)}) copy-start(f32[64,2048]{1,0:T(8,128)} %concatenate.16) | copy-start | bytes 1572868
  86.7 7.5 %copy-start.4 = (f32[64,2048]{1,0:T(8,128)S(1)}, f32[64,2048]{1,0:T(8,128)}, u32[]{:S(2)}) copy-start(f32[64,2048]{1,0:T(8,128)} %concatenate.18) | copy-start | bytes 1572868
  156.7 1.6 copy-start.1
  157.0 2.8 %copy-start.5 = (f32[8192]{0:T(1024)S(1)}, f32[8192]{0:T(1024)}, u32[]{:S(2)}) copy-start(f32[8192]{0:T(1024)} %param.11) | copy-start | bytes 98308
where the time goes:
time: 166 us; the launch traced here: 163 us
  blocking collectives  57.6 us (35%)
  local copies, waits for them, and re-layouts  44.7 us (27%)
  other arithmetic  38.2 us (23%)
  starting transfers between devices  12.3 us (7%)
  matrix products  9.41 us (6%)
    all_to_all x1, blocking collectives, per_device(): lax.all_to_all(mixed_rows, 'chan', split_axis=0, concat_axis=1, tiled=True)  57.6 us
    another operation x2, local copies, waits for them, and re-layouts, serial_rows(): jnp.stack(prod_list, axis=axis_pos)  14.2 us
    another operation x2, local copies, waits for them, and re-layouts, serial_rows(): jnp.stack(state_list, axis=axis_pos)  14.2 us
    all_to_all x1, starting transfers between devices, from_everyone(): lax.all_to_all(jnp.broadcast_to(value[None], (count, *value.shape)), axis...  12.3 us
    add x3, other arithmetic, serial_rows(): state_now = decay_here * state_now + drive_here  9.87 us
    dot_general x3, matrix products, widen(): jnp.dot(head_values, spread_table, preferred_element_type=jnp.float32)  9.41 us
    slice x20, local copies, waits for them, and re-layouts, folded_in_pairs(): part[side::2]  7.43 us
    mul x3, other arithmetic, serial_rows(): prod_now = prod_now * decay_here  5.88 us
  transfers between devices with their start and end apart: 1, of which 0 were waited for; matrix products, arithmetic and copies ran while one was open for 33% of the time, Pallas kernels for 0%

commit v1 on v0

v1 whole, which is shorter than its diff:
```python
import functools

import jax
import jax.numpy as jnp
from jax import lax
from jax.experimental import pallas as pl
from jax.experimental.pallas import tpu as pltpu
from jax.sharding import PartitionSpec as P

MESH = pl.DeviceIdType.MESH
norm_epsilon = 1e-05
LOG2E = 1.4426950408889634

TOK = 512
SUB = 128
CH = 2048
N = 8192
HL = 16
HEADS = 64
GR = 16
NG = SUB // GR
FIRST = 3
SECOND = 8


def drive_factor(widened):
    t = jnp.tanh(widened)
    two_t = t + t
    return two_t * lax.rsqrt(two_t + two_t * t + 1e-37)


def scan_rows(a, b, row):
    for s in (1, 2, 4):
        keep = row >= s
        b = b + a * jnp.where(keep, pltpu.roll(b, s, 0), 0.0)
        a = a * jnp.where(keep, pltpu.roll(a, s, 0), 1.0)
    return a, b


def kernel(
    x_hbm, gate_hbm, steps_hbm, rates_hbm, skip_hbm, gain_hbm, out_hbm,
    x_local, x_all, gate, steps, steps_all, rates, skip, gain,
    spread, later, wide, rest, ends, falls, carry_box, start_box, start_all,
    decay, factor, silu, carry, gated, result,
    local_sem, out_sem, bulk_send, bulk_recv, step_send, step_recv,
    carry_send, carry_recv, start_send, start_recv,
):
    tm, chan = lax.axis_index("tm"), lax.axis_index("chan")
    places = (tm % 4, (tm // 4) % 4, tm // 16)
    strides = (1, 4, 16)

    def chan_peer(r):
        return ((chan // 2 + r // 2) % 2) * 2 + (chan % 2 + r % 2) % 2

    def tm_peer(stage, r):
        here = places[stage]
        return tm + ((here + r) % 4 - here) * strides[stage]

    barrier = pltpu.get_barrier_semaphore()
    for r in (1, 2, 3):
        pl.semaphore_signal(
            barrier, inc=1, device_id={"tm": tm, "chan": chan_peer(r)}, device_id_type=MESH
        )
        for stage in range(3):
            pl.semaphore_signal(
                barrier, inc=1, device_id={"tm": tm_peer(stage, r), "chan": chan}, device_id_type=MESH
            )

    my_cols = pl.ds(pl.multiple_of(chan * CH, CH), CH)
    my_rows = pl.ds(pl.multiple_of(chan * SUB, SUB), SUB)
    load_x = pltpu.make_async_copy(x_hbm, x_local, local_sem.at[0])
    load_steps = pltpu.make_async_copy(steps_hbm, steps, local_sem.at[1])
    load_rates = pltpu.make_async_copy(rates_hbm, rates, local_sem.at[2])
    load_own = pltpu.make_async_copy(x_hbm.at[my_rows], x_all.at[:, my_cols], local_sem.at[3])
    load_gate = pltpu.make_async_copy(gate_hbm, gate, local_sem.at[4])
    load_skip = pltpu.make_async_copy(skip_hbm, skip, local_sem.at[5])
    load_gain = pltpu.make_async_copy(gain_hbm, gain, local_sem.at[6])
    load_own_steps = pltpu.make_async_copy(
        steps_hbm.at[my_rows], steps_all.at[chan], local_sem.at[7]
    )
    for load in (load_x, load_steps, load_rates, load_own, load_own_steps, load_gate, load_skip, load_gain):
        load.start()

    spread[...] = jnp.where(
        lax.broadcasted_iota(jnp.int32, (HL, CH), 1) // 128
        == lax.broadcasted_iota(jnp.int32, (HL, CH), 0),
        1.0,
        0.0,
    ).astype(jnp.bfloat16)
    later[...] = jnp.where(
        lax.broadcasted_iota(jnp.int32, (SUB, SUB), 1)
        > lax.broadcasted_iota(jnp.int32, (SUB, SUB), 0),
        1.0,
        0.0,
    ).astype(jnp.bfloat16)

    load_x.wait()
    load_steps.wait()
    pl.semaphore_wait(barrier, 12)

    def bulk(r, g):
        peer = chan_peer(r)
        return pltpu.make_async_remote_copy(
            src_ref=x_local.at[pl.ds(pl.multiple_of(peer * SUB + g * GR, GR), GR)],
            dst_ref=x_all.at[pl.ds(g * GR, GR), my_cols],
            send_sem=bulk_send.at[r - 1, g],
            recv_sem=bulk_recv.at[r - 1, g],
            device_id={"tm": tm, "chan": peer},
            device_id_type=MESH,
        )

    def step_copy(r):
        peer = chan_peer(r)
        return pltpu.make_async_remote_copy(
            src_ref=steps.at[pl.ds(pl.multiple_of(peer * SUB, SUB), SUB)],
            dst_ref=steps_all.at[chan],
            send_sem=step_send.at[r - 1],
            recv_sem=step_recv.at[r - 1],
            device_id={"tm": tm, "chan": peer},
            device_id_type=MESH,
        )

    far = [(r, g) for g in range(NG) for r in (2, 3)]
    for r in (1, 2, 3):
        step_copy(r).start()
    for r, g in far[:FIRST]:
        bulk(r, g).start()
    for g in range(NG):
        bulk(1, g).start()

    load_rates.wait()

    def summary(j, _):
        base = pl.multiple_of(j * SUB, SUB)
        here = steps[pl.ds(base, SUB), :]
        for c in range(0, CH, 512):
            w = jnp.dot(here, spread[:, c : c + 512], preferred_element_type=jnp.float32)
            wide[:, c : c + 512] = w
            rest[:, c : c + 512] = jnp.dot(
                later[...], w.astype(jnp.bfloat16), preferred_element_type=jnp.float32
            )

        def head(h, _):
            cols = pl.ds(pl.multiple_of(h * 128, 128), 128)
            rate = rates[pl.ds(chan * HL + h, 1), :]
            w, after = wide[:, cols], rest[:, cols]
            x = x_local[pl.ds(base, SUB), cols].astype(jnp.float32)
            term = jnp.exp2(after * (rate * -LOG2E)) * drive_factor(w * rate) * x
            ends[j, pl.ds(h, 1), :] = jnp.sum(term, axis=0, keepdims=True)
            falls[j, pl.ds(h, 1), :] = jnp.exp2((w[0:1] + after[0:1]) * (rate * -LOG2E))
            return 0

        return lax.fori_loop(0, HL, head, 0)

    lax.fori_loop(0, 4, summary, 0)

    e, d = ends[0], falls[0]
    for j in range(1, 4):
        e, d = ends[j] + falls[j] * e, falls[j] * d

    def carry_copy(stage, r):
        here = places[stage]
        return pltpu.make_async_remote_copy(
            src_ref=carry_box.at[stage, here],
            dst_ref=carry_box.at[stage, here],
            send_sem=carry_send.at[stage, r - 1],
            recv_sem=carry_recv.at[stage, r - 1],
            device_id={"tm": tm_peer(stage, r), "chan": chan},
            device_id_type=MESH,
        )

    def carry_arrival(stage, r):
        there = (places[stage] - r + 4) % 4
        return pltpu.make_async_remote_copy(
            src_ref=carry_box.at[stage, there],
            dst_ref=carry_box.at[stage, there],
            send_sem=carry_send.at[stage, r - 1],
            recv_sem=carry_recv.at[stage, r - 1],
            device_id={"tm": tm_peer(stage, r), "chan": chan},
            device_id_type=MESH,
        )

    before = []
    for stage in range(3):
        here = places[stage]
        carry_box[stage, here, 0] = e
        carry_box[stage, here, 1] = d
        for r in (1, 2, 3):
            carry_copy(stage, r).start()
        if stage == 0:
            for r, g in far[FIRST:SECOND]:
                bulk(r, g).start()
        for r in (1, 2, 3):
            carry_arrival(stage, r).wait_recv()
        pre_e, pre_d = jnp.zeros((HL, 128), jnp.float32), jnp.ones((HL, 128), jnp.float32)
        e, d = pre_e, pre_d
        for p in range(4):
            e_p, d_p = carry_box[stage, p, 0], carry_box[stage, p, 1]
            passed = jnp.full((HL, 128), p, jnp.int32) < here
            pre_e = jnp.where(passed, d_p * pre_e + e_p, pre_e)
            pre_d = jnp.where(passed, d_p * pre_d, pre_d)
            e, d = d_p * e + e_p, d_p * d
        before.append((pre_e, pre_d))
    incoming = before[2][0]
    incoming = before[1][1] * incoming + before[1][0]
    incoming = before[0][1] * incoming + before[0][0]

    now = incoming
    for j in range(4):
        start_box[j] = now
        now = falls[j] * now + ends[j]

    def start_copy(r):
        peer = chan_peer(r)
        return pltpu.make_async_remote_copy(
            src_ref=start_box.at[peer],
            dst_ref=start_all.at[chan],
            send_sem=start_send.at[r - 1],
            recv_sem=start_recv.at[r - 1],
            device_id={"tm": tm, "chan": peer},
            device_id_type=MESH,
        )

    start_all[chan] = start_box[chan]
    for r in (1, 2, 3):
        start_copy(r).start()
    for r, g in far[SECOND:]:
        bulk(r, g).start()

    load_own_steps.wait()
    load_gate.wait()
    load_skip.wait()
    load_gain.wait()
    for r in (1, 2, 3):
        step_copy(r).wait_recv()

    def prepare(i, _):
        k, c = i // 4, (i % 4) * 512
        w = jnp.dot(
            steps_all[k],
            spread[:, pl.ds(pl.multiple_of(c, 512), 512)],
            preferred_element_type=jnp.float32,
        )
        for q in range(4):
            cols = pl.ds(pl.multiple_of(i * 512 + q * 128, 128), 128)
            rate = rates[pl.ds(i * 4 + q, 1), :]
            widened = w[:, q * 128 : q * 128 + 128] * rate
            decay[:, cols] = jnp.exp2(widened * -LOG2E)
            factor[:, cols] = drive_factor(widened)
            half = gate[:, cols].astype(jnp.float32) * 0.5
            silu[:, cols] = half + half * jnp.tanh(half)
        return 0

    lax.fori_loop(0, 16, prepare, 0)

    for r in (1, 2, 3):
        start_copy(r).wait_recv()
    load_own.wait()
    for k in range(4):
        carry[k * HL : (k + 1) * HL, :] = start_all[k]

    row = lax.broadcasted_iota(jnp.int32, (8, 128), 0)

    for g in range(NG):
        for r in (1, 2, 3):
            bulk(r, g).wait_recv()
        rows = slice(g * GR, (g + 1) * GR)

        def head(h, total, rows=rows):
            cols = pl.ds(pl.multiple_of(h * 128, 128), 128)
            x = x_all[rows, cols].astype(jnp.float32)
            a = decay[rows, cols]
            b = factor[rows, cols] * x
            state = carry[pl.ds(h, 1), :]
            parts = []
            for p in range(0, GR, 8):
                a_p, b_p = scan_rows(a[p : p + 8], b[p : p + 8], row)
                s_p = b_p + a_p * state
                state = s_p[7:8]
                parts.append(s_p)
            carry[pl.ds(h, 1), :] = state
            s = jnp.concatenate(parts, axis=0)
            mixed = (s + skip[pl.ds(h, 1), :] * x).astype(jnp.bfloat16).astype(jnp.float32)
            v = mixed * silu[rows, cols]
            gated[:, cols] = v
            return total + v * v

        total = lax.fori_loop(0, HEADS, head, jnp.zeros((GR, 128), jnp.float32), unroll=4)
        mean = jnp.sum(total, axis=1, keepdims=True) * (1.0 / N)
        scale = jnp.broadcast_to(lax.rsqrt(mean + norm_epsilon), (GR, 128))

        def finish(h, _, rows=rows, scale=scale):
            cols = pl.ds(pl.multiple_of(h * 128, 128), 128)
            value = gated[:, cols] * scale * gain[pl.ds(h, 1), :]
            result[rows, cols] = value.astype(jnp.bfloat16)
            return 0

        lax.fori_loop(0, HEADS, finish, 0, unroll=8)
        pltpu.make_async_copy(result.at[rows], out_hbm.at[rows], out_sem.at[g]).start()

    for r in (1, 2, 3):
        step_copy(r).wait_send()
        start_copy(r).wait_send()
        for stage in range(3):
            carry_copy(stage, r).wait_send()
        for g in range(NG):
            bulk(r, g).wait_send()
    for g in range(NG):
        rows = slice(g * GR, (g + 1) * GR)
        pltpu.make_async_copy(result.at[rows], out_hbm.at[rows], out_sem.at[g]).wait()


def per_device(inputs, gate_logits, step_sizes, decay_rates, skip_gain, norm_gain):
    f32, bf16, dma = jnp.float32, jnp.bfloat16, pltpu.SemaphoreType.DMA
    any_spec = pl.BlockSpec(memory_space=pl.ANY)
    return pl.pallas_call(
        kernel,
        out_shape=jax.ShapeDtypeStruct((SUB, N), bf16),
        in_specs=[any_spec] * 6,
        out_specs=any_spec,
        scratch_shapes=[
            pltpu.VMEM((TOK, CH), bf16),
            pltpu.VMEM((SUB, N), bf16),
            pltpu.VMEM((SUB, N), bf16),
            pltpu.VMEM((TOK, HL), bf16),
            pltpu.VMEM((4, SUB, HL), bf16),
            pltpu.VMEM((HEADS, 128), f32),
            pltpu.VMEM((HEADS, 128), f32),
            pltpu.VMEM((HEADS, 128), f32),
            pltpu.VMEM((HL, CH), bf16),
            pltpu.VMEM((SUB, SUB), bf16),
            pltpu.VMEM((SUB, CH), f32),
            pltpu.VMEM((SUB, CH), f32),
            pltpu.VMEM((4, HL, 128), f32),
            pltpu.VMEM((4, HL, 128), f32),
            pltpu.VMEM((3, 4, 2, HL, 128), f32),
            pltpu.VMEM((4, HL, 128), f32),
            pltpu.VMEM((4, HL, 128), f32),
            pltpu.VMEM((SUB, N), f32),
            pltpu.VMEM((SUB, N), f32),
            pltpu.VMEM((SUB, N), f32),
            pltpu.VMEM((HEADS, 128), f32),
            pltpu.VMEM((GR, N), f32),
            pltpu.VMEM((SUB, N), bf16),
            dma((8,)),
            dma((NG,)),
            dma((3, NG)),
            dma((3, NG)),
            dma((3,)),
            dma((3,)),
            dma((3, 3)),
            dma((3, 3)),
            dma((3,)),
            dma((3,)),
        ],
        compiler_params=pltpu.CompilerParams(
            collective_id=0, has_side_effects=True, vmem_limit_bytes=56 * 1024 * 1024
        ),
        name="recurrence",
    )(
        inputs,
        gate_logits,
        step_sizes,
        decay_rates.reshape(HEADS, 128),
        skip_gain.reshape(HEADS, 128),
        norm_gain.reshape(HEADS, 128),
    )


def solution(mesh):
    in_specs = (P("tm", "chan"), P(("tm", "chan"), None), P("tm", "chan"), P(), P(), P())
    out_specs = P(("tm", "chan"), None)
    return jax.shard_map(
        per_device, mesh=mesh, in_specs=in_specs, out_specs=out_specs, check_vma=False
    )
```

time: 166 us -> 80.8 us (0.49)
  the two profiles are of different devices: /device:TPU:2 before, /device:TPU:225 now
where the time goes in v1:
time: 80.8 us; the launch traced here: 80.7 us
  Pallas kernels  76.1 us (94%)
  local copies, waits for them, and re-layouts  4.57 us (6%)
    pallas_call x1, Pallas kernels, per_device(): pl.pallas_call(kernel, out_shape=jax.ShapeDtypeStruct((SUB, N), bf16), in...  76.1 us
    unnamed x2, local copies, waits for them, and re-layouts  4.57 us

profile of v1, /device:TPU:225, one launch (start us, length us, event | category | flops | bytes accessed | tf_op | source)
XLA Modules:
  0.0 80.7 jit_solution(17220750742822239925)
XLA Ops:
  0.0 1.5 %copy.7.steps_hbm = bf16[512,16]{1,0:T(8,128)(2,1)} copy(bf16[512,16]{0,1:T(8,128)(2,1)} %param.8) | data formatting | bytes 32768 | tf_op args[2]
  1.5 76.1 %recurrence.1 = bf16[128,8192]{1,0:T(8,128)(2,1)} custom-call(bf16[512,2048]{1,0:T(8,128)(2,1)} %x_hbm.1, bf16[128,8192]{1,0:T(8,128)(2,1)} %gate_hbm.1, bf16[512,16]{1,0:T(8,128)(2,1)} %copy.7.steps_hbm, f32[64,128]{1,0:T(8,128)} %bitcast.3, f32[64,128]{1,0:T(8,128)} %bitcast.4, f32[64,128]{1,0:T(8,128)} %bitcast.5), custom_call_target="tpu_custom_call" | custom-call | tf_op jit(solution)/shard_map/recurrence/pallas_call | solution.py:316
  77.6 3.1 %copy.9 = bf16[128,8192]{1,0:T(8,128)(2,1)} copy(bf16[128,8192]{1,0:T(8,128)(2,1)} %recurrence.1) | data formatting | bytes 4194304

commit v2 on v1

--- a/solution.py
+++ b/solution.py
@@ -19,14 +19,20 @@
 HEADS = 64
 GR = 16
 NG = SUB // GR
-FIRST = 3
-SECOND = 8
+FIRST = 2
+PREP = 7
 
 
 def drive_factor(widened):
     t = jnp.tanh(widened)
     two_t = t + t
     return two_t * lax.rsqrt(two_t + two_t * t + 1e-37)
+
+
+def widen(head_steps, table):
+    return lax.dot_general(
+        head_steps, table, (((0,), (0,)), ((), ())), preferred_element_type=jnp.float32
+    )
 
 
 def scan_rows(a, b, row):
@@ -38,12 +44,12 @@
 
 
 def kernel(
-    x_hbm, gate_hbm, steps_hbm, rates_hbm, skip_hbm, gain_hbm, out_hbm,
+    x_hbm, gate_hbm, steps_hbm, rates_hbm, skip_hbm, gain_hbm, result,
     x_local, x_all, gate, steps, steps_all, rates, skip, gain,
-    spread, later, wide, rest, ends, falls, carry_box, start_box, start_all,
-    decay, factor, silu, carry, gated, result,
-    local_sem, out_sem, bulk_send, bulk_recv, step_send, step_recv,
-    carry_send, carry_recv, start_send, start_recv,
+    spread, by_token, wide, rest, ends, falls, carry_box, start_box, start_all,
+    decay, factor, silu, carry, gated,
+    local_sem, bulk_send, bulk_recv, step_send, step_recv,
+    carry_send, carry_recv, relay_send, relay_recv, start_send, start_recv,
 ):
     tm, chan = lax.axis_index("tm"), lax.axis_index("chan")
     places = (tm % 4, (tm // 4) % 4, tm // 16)
@@ -76,26 +82,38 @@
     load_skip = pltpu.make_async_copy(skip_hbm, skip, local_sem.at[5])
     load_gain = pltpu.make_async_copy(gain_hbm, gain, local_sem.at[6])
     load_own_steps = pltpu.make_async_copy(
-        steps_hbm.at[my_rows], steps_all.at[chan], local_sem.at[7]
+        steps_hbm.at[:, my_rows], steps_all.at[chan], local_sem.at[7]
     )
     for load in (load_x, load_steps, load_rates, load_own, load_own_steps, load_gate, load_skip, load_gain):
         load.start()
 
-    spread[...] = jnp.where(
-        lax.broadcasted_iota(jnp.int32, (HL, CH), 1) // 128
-        == lax.broadcasted_iota(jnp.int32, (HL, CH), 0),
+    for p in range(3):
+        spread[p * HL : (p + 1) * HL, :] = jnp.where(
+            lax.broadcasted_iota(jnp.int32, (HL, CH), 1) // 128
+            == lax.broadcasted_iota(jnp.int32, (HL, CH), 0),
+            1.0,
+            0.0,
+        ).astype(jnp.bfloat16)
+    later = jnp.where(
+        lax.broadcasted_iota(jnp.int32, (SUB, SUB), 0)
+        > lax.broadcasted_iota(jnp.int32, (SUB, SUB), 1),
         1.0,
         0.0,
     ).astype(jnp.bfloat16)
-    later[...] = jnp.where(
-        lax.broadcasted_iota(jnp.int32, (SUB, SUB), 1)
-        > lax.broadcasted_iota(jnp.int32, (SUB, SUB), 0),
-        1.0,
-        0.0,
-    ).astype(jnp.bfloat16)
+
+    load_steps.wait()
+    for j in range(4):
+        here = slice(j * SUB, (j + 1) * SUB)
+        own = steps[:, here]
+        after = jnp.dot(own, later, preferred_element_type=jnp.float32)
+        pieces = []
+        for _ in range(3):
+            pieces.append(after.astype(jnp.bfloat16).astype(jnp.float32))
+            after = after - pieces[-1]
+        turned = jnp.concatenate([own.astype(jnp.float32), *pieces], axis=0).T
+        by_token[here, :] = turned.astype(jnp.bfloat16)
 
     load_x.wait()
-    load_steps.wait()
     pl.semaphore_wait(barrier, 12)
 
     def bulk(r, g):
@@ -112,7 +130,7 @@
     def step_copy(r):
         peer = chan_peer(r)
         return pltpu.make_async_remote_copy(
-            src_ref=steps.at[pl.ds(pl.multiple_of(peer * SUB, SUB), SUB)],
+            src_ref=steps.at[:, pl.ds(pl.multiple_of(peer * SUB, SUB), SUB)],
             dst_ref=steps_all.at[chan],
             send_sem=step_send.at[r - 1],
             recv_sem=step_recv.at[r - 1],
@@ -123,59 +141,93 @@
     far = [(r, g) for g in range(NG) for r in (2, 3)]
     for r in (1, 2, 3):
         step_copy(r).start()
-    for r, g in far[:FIRST]:
-        bulk(r, g).start()
+    started, left = [], []
+
+    def send(count):
+        for r, g in far[len(started) : len(started) + count]:
+            bulk(r, g).start()
+            started.append((r, g))
+
+    def pump(count):
+        for _ in range(count):
+            r, g = started[len(left)]
+            bulk(r, g).wait_send()
+            left.append((r, g))
+            send(1)
+
+    send(FIRST)
     for g in range(NG):
         bulk(1, g).start()
 
+    def widen_block(i, _):
+        cols = pl.ds(pl.multiple_of(i * 256, 256), 256)
+        wide[:, cols] = jnp.dot(
+            by_token[:, :HL], spread[:HL, cols], preferred_element_type=jnp.float32
+        )
+        rest[:, cols] = jnp.dot(
+            by_token[:, HL:], spread[:, cols], preferred_element_type=jnp.float32
+        )
+        return 0
+
+    lax.fori_loop(0, CH // 256, widen_block, 0)
+
     load_rates.wait()
 
     def summary(j, _):
         base = pl.multiple_of(j * SUB, SUB)
-        here = steps[pl.ds(base, SUB), :]
-        for c in range(0, CH, 512):
-            w = jnp.dot(here, spread[:, c : c + 512], preferred_element_type=jnp.float32)
-            wide[:, c : c + 512] = w
-            rest[:, c : c + 512] = jnp.dot(
-                later[...], w.astype(jnp.bfloat16), preferred_element_type=jnp.float32
-            )
-
         def head(h, _):
             cols = pl.ds(pl.multiple_of(h * 128, 128), 128)
             rate = rates[pl.ds(chan * HL + h, 1), :]
-            w, after = wide[:, cols], rest[:, cols]
+            w, after = wide[pl.ds(base, SUB), cols], rest[pl.ds(base, SUB), cols]
             x = x_local[pl.ds(base, SUB), cols].astype(jnp.float32)
             term = jnp.exp2(after * (rate * -LOG2E)) * drive_factor(w * rate) * x
             ends[j, pl.ds(h, 1), :] = jnp.sum(term, axis=0, keepdims=True)
             falls[j, pl.ds(h, 1), :] = jnp.exp2((w[0:1] + after[0:1]) * (rate * -LOG2E))
             return 0
 
-        return lax.fori_loop(0, HL, head, 0)
+        return lax.fori_loop(0, HL, head, 0, unroll=4)
 
     lax.fori_loop(0, 4, summary, 0)
+
+    def prepare(i, _):
+        k, c = i // 4, (i % 4) * 512
+        w = widen(steps_all[k], spread[:HL, pl.ds(pl.multiple_of(c, 512), 512)])
+        for q in range(4):
+            cols = pl.ds(pl.multiple_of(i * 512 + q * 128, 128), 128)
+            rate = rates[pl.ds(i * 4 + q, 1), :]
+            widened = w[:, q * 128 : q * 128 + 128] * rate
+            decay[:, cols] = jnp.exp2(widened * -LOG2E)
+            factor[:, cols] = drive_factor(widened)
+            half = gate[:, cols].astype(jnp.float32) * 0.5
+            silu[:, cols] = half + half * jnp.tanh(half)
+        return 0
+
 
     e, d = ends[0], falls[0]
     for j in range(1, 4):
         e, d = ends[j] + falls[j] * e, falls[j] * d
 
-    def carry_copy(stage, r):
-        here = places[stage]
+    z_lo = places[0]
+
+    def relay_copy(slot, to, at):
         return pltpu.make_async_remote_copy(
-            src_ref=carry_box.at[stage, here],
-            dst_ref=carry_box.at[stage, here],
-            send_sem=carry_send.at[stage, r - 1],
-            recv_sem=carry_recv.at[stage, r - 1],
-            device_id={"tm": tm_peer(stage, r), "chan": chan},
+            src_ref=carry_box.at[0, slot],
+            dst_ref=carry_box.at[0, slot],
+            send_sem=relay_send.at[at],
+            recv_sem=relay_recv.at[slot],
+            device_id={"tm": tm - z_lo + to, "chan": chan},
             device_id_type=MESH,
         )
 
-    def carry_arrival(stage, r):
-        there = (places[stage] - r + 4) % 4
+    own_sends = {0: (1, 2, 3), 1: (0,), 2: (3,), 3: (2, 1, 0)}
+    relays = {0: (1, (2, 3)), 1: (0, ()), 2: (3, ()), 3: (2, (1, 0))}
+
+    def carry_copy(stage, r, slot):
         return pltpu.make_async_remote_copy(
-            src_ref=carry_box.at[stage, there],
-            dst_ref=carry_box.at[stage, there],
-            send_sem=carry_send.at[stage, r - 1],
-            recv_sem=carry_recv.at[stage, r - 1],
+            src_ref=carry_box.at[stage, slot],
+            dst_ref=carry_box.at[stage, slot],
+            send_sem=carry_send.at[stage - 1, r - 1],
+            recv_sem=carry_recv.at[stage - 1, r - 1],
             device_id={"tm": tm_peer(stage, r), "chan": chan},
             device_id_type=MESH,
         )
@@ -185,13 +237,45 @@
         here = places[stage]
         carry_box[stage, here, 0] = e
         carry_box[stage, here, 1] = d
-        for r in (1, 2, 3):
-            carry_copy(stage, r).start()
         if stage == 0:
-            for r, g in far[FIRST:SECOND]:
-                bulk(r, g).start()
-        for r in (1, 2, 3):
-            carry_arrival(stage, r).wait_recv()
+            for place, targets in own_sends.items():
+
+                @pl.when(z_lo == place)
+                def _(place=place, targets=targets):
+                    for at, to in enumerate(targets):
+                        relay_copy(place, to, at).start()
+
+            send(1)
+            load_own_steps.wait()
+            load_gate.wait()
+            for r in (1, 2, 3):
+                step_copy(r).wait_recv()
+            lax.fori_loop(0, PREP, prepare, 0)
+            for place, (slot, targets) in relays.items():
+
+                @pl.when(z_lo == place)
+                def _(slot=slot, targets=targets):
+                    relay_copy(slot, 0, 0).wait_recv()
+                    for at, to in enumerate(targets):
+                        relay_copy(slot, to, 3 + at).start()
+
+            pump(2)
+            send(1)
+            lax.fori_loop(PREP, 16, prepare, 0)
+            for place in range(4):
+
+                @pl.when(z_lo == place)
+                def _(place=place):
+                    for slot in range(4):
+                        if slot not in (place, relays[place][0]):
+                            relay_copy(slot, 0, 0).wait_recv()
+
+        else:
+            for r in (1, 2, 3):
+                carry_copy(stage, r, here).start()
+            pump(1)
+            for r in (1, 2, 3):
+                carry_copy(stage, r, (here - r + 4) % 4).wait_recv()
         pre_e, pre_d = jnp.zeros((HL, 128), jnp.float32), jnp.ones((HL, 128), jnp.float32)
         e, d = pre_e, pre_d
         for p in range(4):
@@ -224,38 +308,13 @@
     start_all[chan] = start_box[chan]
     for r in (1, 2, 3):
         start_copy(r).start()
-    for r, g in far[SECOND:]:
-        bulk(r, g).start()
-
-    load_own_steps.wait()
-    load_gate.wait()
-    load_skip.wait()
-    load_gain.wait()
-    for r in (1, 2, 3):
-        step_copy(r).wait_recv()
-
-    def prepare(i, _):
-        k, c = i // 4, (i % 4) * 512
-        w = jnp.dot(
-            steps_all[k],
-            spread[:, pl.ds(pl.multiple_of(c, 512), 512)],
-            preferred_element_type=jnp.float32,
-        )
-        for q in range(4):
-            cols = pl.ds(pl.multiple_of(i * 512 + q * 128, 128), 128)
-            rate = rates[pl.ds(i * 4 + q, 1), :]
-            widened = w[:, q * 128 : q * 128 + 128] * rate
-            decay[:, cols] = jnp.exp2(widened * -LOG2E)
-            factor[:, cols] = drive_factor(widened)
-            half = gate[:, cols].astype(jnp.float32) * 0.5
-            silu[:, cols] = half + half * jnp.tanh(half)
-        return 0
-
-    lax.fori_loop(0, 16, prepare, 0)
+    send(2 * NG)
 
     for r in (1, 2, 3):
         start_copy(r).wait_recv()
     load_own.wait()
+    load_skip.wait()
+    load_gain.wait()
     for k in range(4):
         carry[k * HL : (k + 1) * HL, :] = start_all[k]
 
@@ -296,41 +355,47 @@
             return 0
 
         lax.fori_loop(0, HEADS, finish, 0, unroll=8)
-        pltpu.make_async_copy(result.at[rows], out_hbm.at[rows], out_sem.at[g]).start()
 
     for r in (1, 2, 3):
         step_copy(r).wait_send()
         start_copy(r).wait_send()
-        for stage in range(3):
-            carry_copy(stage, r).wait_send()
+        for stage in (1, 2):
+            carry_copy(stage, r, places[stage]).wait_send()
         for g in range(NG):
-            bulk(r, g).wait_send()
-    for g in range(NG):
-        rows = slice(g * GR, (g + 1) * GR)
-        pltpu.make_async_copy(result.at[rows], out_hbm.at[rows], out_sem.at[g]).wait()
+            if (r, g) not in left:
+                bulk(r, g).wait_send()
+    for place in range(4):
+
+        @pl.when(z_lo == place)
+        def _(place=place):
+            for at in range(len(own_sends[place])):
+                relay_copy(place, 0, at).wait_send()
+            if len(relays[place][1]):
+                for at in range(2):
+                    relay_copy(place, 0, 3 + at).wait_send()
 
 
 def per_device(inputs, gate_logits, step_sizes, decay_rates, skip_gain, norm_gain):
     f32, bf16, dma = jnp.float32, jnp.bfloat16, pltpu.SemaphoreType.DMA
-    any_spec = pl.BlockSpec(memory_space=pl.ANY)
+    any_spec = pl.BlockSpec(memory_space=pltpu.HBM)
     return pl.pallas_call(
         kernel,
         out_shape=jax.ShapeDtypeStruct((SUB, N), bf16),
         in_specs=[any_spec] * 6,
-        out_specs=any_spec,
+        out_specs=pl.BlockSpec(memory_space=pltpu.VMEM),
         scratch_shapes=[
             pltpu.VMEM((TOK, CH), bf16),
             pltpu.VMEM((SUB, N), bf16),
             pltpu.VMEM((SUB, N), bf16),
-            pltpu.VMEM((TOK, HL), bf16),
-            pltpu.VMEM((4, SUB, HL), bf16),
+            pltpu.VMEM((HL, TOK), bf16),
+            pltpu.VMEM((4, HL, SUB), bf16),
             pltpu.VMEM((HEADS, 128), f32),
             pltpu.VMEM((HEADS, 128), f32),
             pltpu.VMEM((HEADS, 128), f32),
-            pltpu.VMEM((HL, CH), bf16),
-            pltpu.VMEM((SUB, SUB), bf16),
-            pltpu.VMEM((SUB, CH), f32),
-            pltpu.VMEM((SUB, CH), f32),
+            pltpu.VMEM((3 * HL, CH), bf16),
+            pltpu.VMEM((TOK, 4 * HL), bf16),
+            pltpu.VMEM((TOK, CH), f32),
+            pltpu.VMEM((TOK, CH), f32),
             pltpu.VMEM((4, HL, 128), f32),
             pltpu.VMEM((4, HL, 128), f32),
             pltpu.VMEM((3, 4, 2, HL, 128), f32),
@@ -341,29 +406,34 @@
             pltpu.VMEM((SUB, N), f32),
             pltpu.VMEM((HEADS, 128), f32),
             pltpu.VMEM((GR, N), f32),
-            pltpu.VMEM((SUB, N), bf16),
             dma((8,)),
-            dma((NG,)),
             dma((3, NG)),
             dma((3, NG)),
             dma((3,)),
             dma((3,)),
-            dma((3, 3)),
-            dma((3, 3)),
+            dma((2, 3)),
+            dma((2, 3)),
+            dma((5,)),
+            dma((4,)),
             dma((3,)),
             dma((3,)),
         ],
         compiler_params=pltpu.CompilerParams(
-            collective_id=0, has_side_effects=True, vmem_limit_bytes=56 * 1024 * 1024
+            collective_id=0, has_side_effects=True, vmem_limit_bytes=40 * 1024 * 1024
         ),
         name="recurrence",
     )(
-        inputs,
-        gate_logits,
-        step_sizes,
-        decay_rates.reshape(HEADS, 128),
-        skip_gain.reshape(HEADS, 128),
-        norm_gain.reshape(HEADS, 128),
+        *(
+            pltpu.with_memory_space_constraint(operand, pltpu.HBM)
+            for operand in (
+                inputs,
+                gate_logits,
+                step_sizes.T,
+                decay_rates.reshape(HEADS, 128),
+                skip_gain.reshape(HEADS, 128),
+                norm_gain.reshape(HEADS, 128),
+            )
+        )
     )
 
 

time: 80.8 us -> 61.6 us (0.76)
  the two profiles are of different devices: /device:TPU:225 before, /device:TPU:65 now
where the time goes in v2:
time: 61.6 us; the launch traced here: 60.5 us
  Pallas kernels  59.2 us (96%)
  local copies, waits for them, and re-layouts  1.32 us (2%)
    pallas_call x1, Pallas kernels, per_device(): pl.pallas_call(kernel, out_shape=jax.ShapeDtypeStruct((SUB, N), bf16), in...  59.2 us
    unnamed x1, local copies, waits for them, and re-layouts  1.32 us

profile of v2, /device:TPU:65, one launch (start us, length us, event | category | flops | bytes accessed | tf_op | source)
XLA Modules:
  0.0 60.5 jit_solution(5221039343375962326)
XLA Ops:
  0.0 59.2 %recurrence.1 = bf16[128,8192]{1,0:T(8,128)(2,1)S(1)} custom-call(bf16[512,2048]{1,0:T(8,128)(2,1)} %x_hbm.1, bf16[128,8192]{1,0:T(8,128)(2,1)} %gate_hbm.1, bf16[16,512]{1,0:T(8,128)(2,1)} %bitcast.7, f32[64,128]{1,0:T(8,128)} %bitcast.4, f32[64,128]{1,0:T(8,128)} %bitcast.5, f32[64,128]{1,0:T(8,128)} %bitcast.6), custom_call_target="tpu_custom_call" | custom-call | tf_op jit(solution)/shard_map/recurrence/pallas_call | solution.py:381
  59.2 1.3 %copy.8 = bf16[128,8192]{1,0:T(8,128)(2,1)} copy(bf16[128,8192]{1,0:T(8,128)(2,1)S(1)} %recurrence.1) | data formatting | bytes 4194304
